TPU v7x, 32 devices: a whole 2x2x4 slice. The times are simulated.
32 devices in a mesh: ta: 4 (over z), gz: 2 (over x), xy: 4 (over y, core).
Axes of the slice: x: 2, y: 2, z: 4, core: 2. Of those that a mesh axis runs over, the one named last changes fastest.
Arguments:
- links: float32 [4, 2, 4, 4, 9, 4608], P('ta', 'gz', 'xy'), may hold values from -1 to 3
- eigvecs: float32 [4, 2, 4, 4, 48, 128], P('ta', 'gz', 'xy'), may hold values from -1 to 1
- eig_real: float32 [64], replicated, may hold values from 0.8 to 2.5
- eig_imag: float32 [64], replicated, may hold values from -0.5 to 0.5
- rhs: float32 [4, 2, 4, 4, 48, 128], P('ta', 'gz', 'xy'), may hold values from -3000 to 3000
Outputs:
- solution: float32 [4, 2, 4, 4, 48, 128], P('ta', 'gz', 'xy')
- residual: float32 [4, 2, 4, 4, 48, 128], P('ta', 'gz', 'xy')
All inputs are finite; a program needn't handle non-finite values.
Results may differ from a plain program's by a relative error of at most 0.0003.
Values sent between devices are 32-bit elements; how exact they have to be, the bound alone decides.
No kernel may reach another device: no remote copies, remote signals or barrier semaphores. Data moves between devices by JAX's collectives and lax.ppermute only.
A program may use at most 64 MiB of HBM per device.

v0:
```python
import jax
import jax.numpy as jnp
from jax import lax
from jax.sharding import PartitionSpec as P

SWEEPS = 4


HIGH = lax.Precision.HIGHEST


def with_halo(x, sides, width):
    for axis, dim in sides:
        peers, length = (lax.axis_size(axis), x.shape[dim])
        up = [(i, (i + 1) % peers) for i in range(peers)]
        down = [(j, i) for i, j in up]
        last = lax.slice_in_dim(x, length - width, length, axis=dim)
        initial = lax.slice_in_dim(x, 0, width, axis=dim)
        before = lax.ppermute(last, axis, up)
        after = lax.ppermute(initial, axis, down)
        x = jnp.concatenate([before, x, after], axis=dim)
    return x


def operate(links, field):
    dof = field.shape[4]
    half = field.shape[-1] // 2
    padded = with_halo(field, (("ta", 0), ("gz", 1), ("xy", 2)), 1)
    centre = padded[1:-1, 1:-1, 1:-1]
    stacked = jnp.stack(
        [
            centre,
            -padded[2:, 1:-1, 1:-1],
            -padded[1:-1, 2:, 1:-1],
            -padded[1:-1, 1:-1, 2:],
            -jnp.roll(centre, -1, 3),
            -padded[:-2, 1:-1, 1:-1],
            -padded[1:-1, :-2, 1:-1],
            -padded[1:-1, 1:-1, :-2],
            -jnp.roll(centre, 1, 3),
        ],
        4,
    )
    real = jnp.einsum("tzxydoi,tzxydic->tzxyoc", links[..., :dof], stacked, precision=HIGH)
    imag = jnp.einsum("tzxydoi,tzxydic->tzxyoc", links[..., dof:], stacked, precision=HIGH)
    return jnp.concatenate(
        [real[..., :half] - imag[..., half:], real[..., half:] + imag[..., :half]], -1
    )


def complex_scale(alpha_re, alpha_im, field):
    half = field.shape[-1] // 2
    f_re = field[..., :half]
    f_im = field[..., half:]
    return jnp.concatenate(
        [alpha_re * f_re - alpha_im * f_im, alpha_re * f_im + alpha_im * f_re], -1
    )


def sweep_step(image, residual):
    half = residual.shape[-1] // 2
    swapped = jnp.concatenate([residual[..., half:], residual[..., :half]], -1)
    first = jnp.sum(image * residual, axis=(0, 1, 2, 3, 4))
    second = jnp.sum(image * swapped, axis=(0, 1, 2, 3, 4))
    power = jnp.sum(image * image, axis=(0, 1, 2, 3, 4))
    num_re, num_im, den = lax.psum(
        (first[:half] + first[half:], second[:half] - second[half:], power[:half] + power[half:]),
        ("ta", "gz", "xy"),
    )
    return (num_re / den, num_im / den)


def local(links, eigvecs, eig_real, eig_imag, rhs):
    nev = eig_real.shape[0]
    half = rhs.shape[-1] // 2
    dof = rhs.shape[4]
    matrices = links.reshape(links.shape[:5] + (dof, 2 * dof))
    rows = eigvecs.reshape(-1, 2 * nev)
    local_cross = jnp.dot(
        rows.T, rhs.reshape(-1, 2 * half), precision=HIGH, preferred_element_type=jnp.float32
    )
    cross = lax.psum(local_cross, ("ta", "gz", "xy"))
    proj_re = cross[:nev, :half] + cross[nev:, half:]
    proj_im = cross[:nev, half:] - cross[nev:, :half]
    denom = (eig_real * eig_real + eig_imag * eig_imag)[:, None]
    coef_re = (proj_re * eig_real[:, None] + proj_im * eig_imag[:, None]) / denom
    coef_im = (proj_im * eig_real[:, None] - proj_re * eig_imag[:, None]) / denom
    block = jnp.concatenate(
        [jnp.concatenate([coef_re, coef_im], 1), jnp.concatenate([-coef_im, coef_re], 1)], 0
    )
    solution = jnp.dot(rows, block, precision=HIGH, preferred_element_type=jnp.float32).reshape(
        rhs.shape
    )
    residual = rhs - operate(matrices, solution)
    image = operate(matrices, residual)
    for sweep in range(SWEEPS):
        alpha_re, alpha_im = sweep_step(image, residual)
        if sweep + 1 < SWEEPS:
            further = operate(matrices, image)
        solution = solution + complex_scale(alpha_re, alpha_im, residual)
        residual = residual - complex_scale(alpha_re, alpha_im, image)
        if sweep + 1 < SWEEPS:
            image = image - complex_scale(alpha_re, alpha_im, further)
    return (solution, residual)


def solution(mesh):
    in_specs = (
        P("ta", "gz", "xy", None, None, None),
        P("ta", "gz", "xy", None, None, None),
        P(),
        P(),
        P("ta", "gz", "xy", None, None, None),
    )
    out_specs = (P("ta", "gz", "xy", None, None, None), P("ta", "gz", "xy", None, None, None))
    return jax.shard_map(local, mesh=mesh, in_specs=in_specs, out_specs=out_specs, check_vma=False)
```

profile of v0, /device:TPU:0, one launch (start us, length us, event | category | flops | bytes accessed | tf_op | source)
XLA Modules:
  0.0 525.7 jit_solution(15367684334829813068)
XLA Ops:
  8.1 2.0 convolution_bitcast_fusion.10
  10.7 125.6 %all-reduce.6.cloned.1.call-done = f32[128,128]{1,0:T(8,128)} async-done(((f32[128,128]{1,0:T(8,128)}), f32[128,128]{1,0:T(8,128)}) %all-reduce.6.cloned.1.call-update) | async-done | bytes 65552 | tf_op jit(solution)/shard_map/psum | solution.py:82
  137.6 2.9 collective-permute-start.1
  141.9 2.5 collective-permute-done.1
  148.7 7.5 %collective-permute-done.3 = f32[3,1,1,4,48,128]{5,4,3,2,1,0:T(8,128)S(1)} collective-permute-done((f32[3,1,1,4,48,128]{5,4,3,2,1,0:T(8,128)S(1)}, f32[3,1,1,4,48,128]{5,4,3,2,1,0:T(8,128)S(1)}, u32[]{:S(2)}, u32[]{:S(2)}) %collective-permute-start.3) | collective-permute-done | bytes 294944 | tf_op jit(solution)/shard_map/ppermute | solution.py:19
  156.2 4.8 collective-permute-done.2
  161.7 18.4 %collective-permute-done.4 = f32[3,3,1,4,48,128]{5,4,3,2,1,0:T(8,128)S(1)} collective-permute-done((f32[3,3,1,4,48,128]{5,4,3,2,1,0:T(8,128)S(1)}, f32[3,3,1,4,48,128]{5,4,3,2,1,0:T(8,128)S(1)}, u32[]{:S(2)}, u32[]{:S(2)}) %collective-permute-start.4) | collective-permute-done | bytes 884768 | tf_op jit(solution)/shard_map/ppermute | solution.py:20
  180.2 2.9 collective-permute-done.5
  188.2 2.4 collective-permute-start.6
  190.6 3.7 collective-permute-done.7
  197.0 7.8 %collective-permute-done.9 = f32[3,1,1,4,48,128]{5,4,3,2,1,0:T(8,128)S(1)} collective-permute-done((f32[3,1,1,4,48,128]{5,4,3,2,1,0:T(8,128)S(1)}, f32[3,1,1,4,48,128]{5,4,3,2,1,0:T(8,128)S(1)}, u32[]{:S(2)}, u32[]{:S(2)}) %collective-permute-start.9) | collective-permute-done | bytes 294944 | tf_op jit(solution)/shard_map/ppermute | solution.py:19
  204.8 4.5 collective-permute-done.8
  210.1 19.4 %collective-permute-done.10 = f32[3,3,1,4,48,128]{5,4,3,2,1,0:T(8,128)S(1)} collective-permute-done((f32[3,3,1,4,48,128]{5,4,3,2,1,0:T(8,128)S(1)}, f32[3,3,1,4,48,128]{5,4,3,2,1,0:T(8,128)S(1)}, u32[]{:S(2)}, u32[]{:S(2)}) %collective-permute-start.10) | collective-permute-done | bytes 884768 | tf_op jit(solution)/shard_map/ppermute | solution.py:20
  235.6 2.6 collective-permute-done.12
  238.2 3.5 collective-permute-done.13
  244.0 44.6 %all-reduce.3 = (f32[64]{0:T(128)S(1)}, f32[64]{0:T(128)S(1)}, f32[64]{0:T(128)S(1)}) all-reduce(f32[64]{0:T(128)S(1)} %get-tuple-element.116, f32[64]{0:T(128)S(1)} %get-tuple-element.117, f32[64]{0:T(128)S(1)} %slice_add_fusion.13), channel_id=1, replica_groups=mesh['ta'=4,'gz'=2,'xy'=4] {'ta','gz','xy'}, use_global_device_ids=true, to_apply=%region_6.7 | all-reduce | flops 192 | bytes 1536 | tf_op jit(solution)/shard_map/psum | solution.py:66
  289.8 16.9 %collective-permute-done.16 = f32[3,3,1,4,48,128]{5,4,3,2,1,0:T(8,128)S(1)} collective-permute-done((f32[3,3,1,4,48,128]{5,4,3,2,1,0:T(8,128)S(1)}, f32[3,3,1,4,48,128]{5,4,3,2,1,0:T(8,128)S(1)}, u32[]{:S(2)}, u32[]{:S(2)}) %collective-permute-start.16) | collective-permute-done | bytes 884768 | tf_op jit(solution)/shard_map/ppermute | solution.py:20
  306.7 4.8 collective-permute-done.17
  316.2 2.6 collective-permute-start.18
  319.0 37.1 %all-reduce.2 = (f32[64]{0:T(128)S(1)}, f32[64]{0:T(128)S(1)}, f32[64]{0:T(128)S(1)}) all-reduce(f32[64]{0:T(128)S(1)} %slice_subtract_fusion.8, f32[64]{0:T(128)S(1)} %slice_add_fusion.10, f32[64]{0:T(128)S(1)} %slice_add_fusion.11), channel_id=1, replica_groups=mesh['ta'=4,'gz'=2,'xy'=4] {'ta','gz','xy'}, use_global_device_ids=true, to_apply=%region_12.13 | all-reduce | flops 192 | bytes 1536 | tf_op jit(solution)/shard_map/psum | solution.py:66
  356.2 2.3 collective-permute-start.21
  358.7 7.6 %collective-permute-done.21 = f32[3,1,1,4,48,128]{5,4,3,2,1,0:T(8,128)S(1)} collective-permute-done((f32[3,1,1,4,48,128]{5,4,3,2,1,0:T(8,128)S(1)}, f32[3,1,1,4,48,128]{5,4,3,2,1,0:T(8,128)S(1)}, u32[]{:S(2)}, u32[]{:S(2)}) %collective-permute-start.21) | collective-permute-done | bytes 294944 | tf_op jit(solution)/shard_map/ppermute | solution.py:19
  366.4 4.1 collective-permute-done.20
  371.2 18.8 %collective-permute-done.22 = f32[3,3,1,4,48,128]{5,4,3,2,1,0:T(8,128)S(1)} collective-permute-done((f32[3,3,1,4,48,128]{5,4,3,2,1,0:T(8,128)S(1)}, f32[3,3,1,4,48,128]{5,4,3,2,1,0:T(8,128)S(1)}, u32[]{:S(2)}, u32[]{:S(2)}) %collective-permute-start.22) | collective-permute-done | bytes 884768 | tf_op jit(solution)/shard_map/ppermute | solution.py:20
  390.1 2.1 collective-permute-done.23
  395.6 2.6 collective-permute-start.25
  399.7 3.3 collective-permute-done.25
  404.0 2.1 collective-permute-start.27
  406.3 46.3 %all-reduce.1 = (f32[64]{0:T(128)S(1)}, f32[64]{0:T(128)S(1)}, f32[64]{0:T(128)S(1)}) all-reduce(f32[64]{0:T(128)S(1)} %slice_subtract_fusion.7, f32[64]{0:T(128)S(1)} %slice_add_fusion.8, f32[64]{0:T(128)S(1)} %slice_add_fusion.9), channel_id=1, replica_groups=mesh['ta'=4,'gz'=2,'xy'=4] {'ta','gz','xy'}, use_global_device_ids=true, to_apply=%region_18.19 | all-reduce | flops 192 | bytes 1536 | tf_op jit(solution)/shard_map/psum | solution.py:66
  453.7 17.2 %collective-permute-done.28 = f32[3,3,1,4,48,128]{5,4,3,2,1,0:T(8,128)S(1)} collective-permute-done((f32[3,3,1,4,48,128]{5,4,3,2,1,0:T(8,128)S(1)}, f32[3,3,1,4,48,128]{5,4,3,2,1,0:T(8,128)S(1)}, u32[]{:S(2)}, u32[]{:S(2)}) %collective-permute-start.28) | collective-permute-done | bytes 884768 | tf_op jit(solution)/shard_map/ppermute | solution.py:20
  470.9 4.7 collective-permute-done.29
  479.3 37.9 %all-reduce = (f32[64]{0:T(128)S(1)}, f32[64]{0:T(128)S(1)}, f32[64]{0:T(128)S(1)}) all-reduce(f32[64]{0:T(128)S(1)} %slice_subtract_fusion.6, f32[64]{0:T(128)S(1)} %slice_add_fusion.6, f32[64]{0:T(128)S(1)} %slice_add_fusion.7), channel_id=1, replica_groups=mesh['ta'=4,'gz'=2,'xy'=4] {'ta','gz','xy'}, use_global_device_ids=true, to_apply=%region_24.25 | all-reduce | flops 192 | bytes 1536 | tf_op jit(solution)/shard_map/psum | solution.py:66
  (156 shorter events, 45.4 us)
Async XLA Ops:
  7.2 134.3 %copy-start.1 = (f32[1,1,1,4,9,4608]{5,3,4,2,1,0:T(4,128)S(1)}, f32[1,1,1,4,9,4608]{5,3,4,2,1,0:T(4,128)}, u32[]{:S(2)}) copy-start(f32[1,1,1,4,9,4608]{5,3,4,2,1,0:T(4,128)} %param.5) | copy-start | bytes 1990660
  7.2 129.1 %all-reduce.6.cloned.1.call-start = ((), (), s32[]{:S(2)}) async-start(), calls=%async_computation | async-start | bytes 131072 | tf_op jit(solution)/shard_map/psum | solution.py:82
  137.6 6.9 %collective-permute-start.1 = (f32[1,1,1,4,48,128]{5,4,3,2,1,0:T(8,128)S(1)}, f32[1,1,1,4,48,128]{5,4,3,2,1,0:T(8,128)S(1)}, u32[]{:S(2)}, u32[]{:S(2)}) collective-permute-start(f32[1,1,1,4,48,128]{5,4,3,2,1,0:T(8,128)S(1)} %bitcast.301), channel_id=1, source_target_pairs={{0,8},{8,16},{16,24},{24,0},{1,9},{9,17},{17,25},{25,1},{2,10},{10... | collective-permute-start | bytes 294920 | tf_op jit(solution)/shard_map/ppermute | solution.py:19
  140.5 5.7 %collective-permute-start = (f32[1,1,1,4,48,128]{5,4,3,2,1,0:T(8,128)S(1)}, f32[1,1,1,4,48,128]{5,4,3,2,1,0:T(8,128)S(1)}, u32[]{:S(2)}, u32[]{:S(2)}) collective-permute-start(f32[1,1,1,4,48,128]{5,4,3,2,1,0:T(8,128)S(1)} %bitcast.302), channel_id=1, source_target_pairs={{8,0},{16,8},{24,16},{0,24},{9,1},{17,9},{25,17},{1,25},{10,2},{18... | collective-permute-start | bytes 294920 | tf_op jit(solution)/shard_map/ppermute | solution.py:20
  146.3 9.9 %collective-permute-start.3 = (f32[3,1,1,4,48,128]{5,4,3,2,1,0:T(8,128)S(1)}, f32[3,1,1,4,48,128]{5,4,3,2,1,0:T(8,128)S(1)}, u32[]{:S(2)}, u32[]{:S(2)}) collective-permute-start(f32[3,1,1,4,48,128]{5,4,3,2,1,0:T(8,128)S(1)} %pad_maximum_fusion.5), channel_id=1, source_target_pairs={{0,4},{4,0},{1,5},{5,1},{2,6},{6,2},{3,7},{7,3},{8,12},{12,8},{9,1... | collective-permute-start | bytes 884744 | tf_op jit(solution)/shard_map/ppermute | solution.py:19
  147.8 13.2 %collective-permute-start.2 = (f32[3,1,1,4,48,128]{5,4,3,2,1,0:T(8,128)S(1)}, f32[3,1,1,4,48,128]{5,4,3,2,1,0:T(8,128)S(1)}, u32[]{:S(2)}, u32[]{:S(2)}) collective-permute-start(f32[3,1,1,4,48,128]{5,4,3,2,1,0:T(8,128)S(1)} %pad_maximum_fusion.5), channel_id=1, source_target_pairs={{4,0},{0,4},{5,1},{1,5},{6,2},{2,6},{7,3},{3,7},{12,8},{8,12},{13,... | collective-permute-start | bytes 884744 | tf_op jit(solution)/shard_map/ppermute | solution.py:20
  161.1 19.1 %collective-permute-start.4 = (f32[3,3,1,4,48,128]{5,4,3,2,1,0:T(8,128)S(1)}, f32[3,3,1,4,48,128]{5,4,3,2,1,0:T(8,128)S(1)}, u32[]{:S(2)}, u32[]{:S(2)}) collective-permute-start(f32[3,3,1,4,48,128]{5,4,3,2,1,0:T(8,128)S(1)} %pad_maximum_fusion), channel_id=1, source_target_pairs={{1,0},{2,1},{3,2},{0,3},{5,4},{6,5},{7,6},{4,7},{9,8},{10,9},{11,1... | collective-permute-start | bytes 2654216 | tf_op jit(solution)/shard_map/ppermute | solution.py:20
  161.2 21.9 %collective-permute-start.5 = (f32[3,3,1,4,48,128]{5,4,3,2,1,0:T(8,128)S(1)}, f32[3,3,1,4,48,128]{5,4,3,2,1,0:T(8,128)S(1)}, u32[]{:S(2)}, u32[]{:S(2)}) collective-permute-start(f32[3,3,1,4,48,128]{5,4,3,2,1,0:T(8,128)S(1)} %pad_maximum_fusion), channel_id=1, source_target_pairs={{0,1},{1,2},{2,3},{3,0},{4,5},{5,6},{6,7},{7,4},{8,9},{9,10},{10,1... | collective-permute-start | bytes 2654216 | tf_op jit(solution)/shard_map/ppermute | solution.py:19
  186.7 7.6 %collective-permute-start.7 = (f32[1,1,1,4,48,128]{5,4,3,2,1,0:T(8,128)S(1)}, f32[1,1,1,4,48,128]{5,4,3,2,1,0:T(8,128)S(1)}, u32[]{:S(2)}, u32[]{:S(2)}) collective-permute-start(f32[1,1,1,4,48,128]{5,4,3,2,1,0:T(8,128)S(1)} %get-tuple-element.34), channel_id=1, source_target_pairs={{0,8},{8,16},{16,24},{24,0},{1,9},{9,17},{17,25},{25,1},{2,10},{10... | collective-permute-start | bytes 294920 | tf_op jit(solution)/shard_map/ppermute | solution.py:19
  188.2 6.6 %collective-permute-start.6 = (f32[1,1,1,4,48,128]{5,4,3,2,1,0:T(8,128)S(1)}, f32[1,1,1,4,48,128]{5,4,3,2,1,0:T(8,128)S(1)}, u32[]{:S(2)}, u32[]{:S(2)}) collective-permute-start(f32[1,1,1,4,48,128]{5,4,3,2,1,0:T(8,128)S(1)} %get-tuple-element.34), channel_id=1, source_target_pairs={{8,0},{16,8},{24,16},{0,24},{9,1},{17,9},{25,17},{1,25},{10,2},{18... | collective-permute-start | bytes 294920 | tf_op jit(solution)/shard_map/ppermute | solution.py:20
  194.9 9.9 %collective-permute-start.9 = (f32[3,1,1,4,48,128]{5,4,3,2,1,0:T(8,128)S(1)}, f32[3,1,1,4,48,128]{5,4,3,2,1,0:T(8,128)S(1)}, u32[]{:S(2)}, u32[]{:S(2)}) collective-permute-start(f32[3,1,1,4,48,128]{5,4,3,2,1,0:T(8,128)S(1)} %pad_maximum_fusion.6), channel_id=1, source_target_pairs={{0,4},{4,0},{1,5},{5,1},{2,6},{6,2},{3,7},{7,3},{8,12},{12,8},{9,1... | collective-permute-start | bytes 884744 | tf_op jit(solution)/shard_map/ppermute | solution.py:19
  196.1 13.2 %collective-permute-start.8 = (f32[3,1,1,4,48,128]{5,4,3,2,1,0:T(8,128)S(1)}, f32[3,1,1,4,48,128]{5,4,3,2,1,0:T(8,128)S(1)}, u32[]{:S(2)}, u32[]{:S(2)}) collective-permute-start(f32[3,1,1,4,48,128]{5,4,3,2,1,0:T(8,128)S(1)} %pad_maximum_fusion.6), channel_id=1, source_target_pairs={{4,0},{0,4},{5,1},{1,5},{6,2},{2,6},{7,3},{3,7},{12,8},{8,12},{13,... | collective-permute-start | bytes 884744 | tf_op jit(solution)/shard_map/ppermute | solution.py:20
  209.3 20.1 %collective-permute-start.10 = (f32[3,3,1,4,48,128]{5,4,3,2,1,0:T(8,128)S(1)}, f32[3,3,1,4,48,128]{5,4,3,2,1,0:T(8,128)S(1)}, u32[]{:S(2)}, u32[]{:S(2)}) collective-permute-start(f32[3,3,1,4,48,128]{5,4,3,2,1,0:T(8,128)S(1)} %pad_maximum_fusion.1), channel_id=1, source_target_pairs={{1,0},{2,1},{3,2},{0,3},{5,4},{6,5},{7,6},{4,7},{9,8},{10,9},{11,1... | collective-permute-start | bytes 2654216 | tf_op jit(solution)/shard_map/ppermute | solution.py:20
  209.5 20.7 %collective-permute-start.11 = (f32[3,3,1,4,48,128]{5,4,3,2,1,0:T(8,128)S(1)}, f32[3,3,1,4,48,128]{5,4,3,2,1,0:T(8,128)S(1)}, u32[]{:S(2)}, u32[]{:S(2)}) collective-permute-start(f32[3,3,1,4,48,128]{5,4,3,2,1,0:T(8,128)S(1)} %pad_maximum_fusion.1), channel_id=1, source_target_pairs={{0,1},{1,2},{2,3},{3,0},{4,5},{5,6},{6,7},{7,4},{8,9},{9,10},{10,1... | collective-permute-start | bytes 2654216 | tf_op jit(solution)/shard_map/ppermute | solution.py:19
  233.4 4.8 collective-permute-start.12
  235.3 6.4 %collective-permute-start.13 = (f32[1,1,1,4,48,128]{5,4,3,2,1,0:T(8,128)S(1)}, f32[1,1,1,4,48,128]{5,4,3,2,1,0:T(8,128)S(1)}, u32[]{:S(2)}, u32[]{:S(2)}) collective-permute-start(f32[1,1,1,4,48,128]{5,4,3,2,1,0:T(8,128)S(1)} %get-tuple-element.32), channel_id=1, source_target_pairs={{0,8},{8,16},{16,24},{24,0},{1,9},{9,17},{17,25},{25,1},{2,10},{10... | collective-permute-start | bytes 294920 | tf_op jit(solution)/shard_map/ppermute | solution.py:19
  241.8 46.8 %collective-permute-start.15 = (f32[3,1,1,4,48,128]{5,4,3,2,1,0:T(8,128)S(1)}, f32[3,1,1,4,48,128]{5,4,3,2,1,0:T(8,128)S(1)}, u32[]{:S(2)}, u32[]{:S(2)}) collective-permute-start(f32[3,1,1,4,48,128]{5,4,3,2,1,0:T(8,128)S(1)} %pad_maximum_fusion.7), channel_id=1, source_target_pairs={{0,4},{4,0},{1,5},{5,1},{2,6},{6,2},{3,7},{7,3},{8,12},{12,8},{9,1... | collective-permute-start | bytes 884744 | tf_op jit(solution)/shard_map/ppermute | solution.py:19
  243.6 45.0 %collective-permute-start.14 = (f32[3,1,1,4,48,128]{5,4,3,2,1,0:T(8,128)S(1)}, f32[3,1,1,4,48,128]{5,4,3,2,1,0:T(8,128)S(1)}, u32[]{:S(2)}, u32[]{:S(2)}) collective-permute-start(f32[3,1,1,4,48,128]{5,4,3,2,1,0:T(8,128)S(1)} %pad_maximum_fusion.7), channel_id=1, source_target_pairs={{4,0},{0,4},{5,1},{1,5},{6,2},{2,6},{7,3},{3,7},{12,8},{8,12},{13,... | collective-permute-start | bytes 884744 | tf_op jit(solution)/shard_map/ppermute | solution.py:20
  288.7 17.9 %collective-permute-start.16 = (f32[3,3,1,4,48,128]{5,4,3,2,1,0:T(8,128)S(1)}, f32[3,3,1,4,48,128]{5,4,3,2,1,0:T(8,128)S(1)}, u32[]{:S(2)}, u32[]{:S(2)}) collective-permute-start(f32[3,3,1,4,48,128]{5,4,3,2,1,0:T(8,128)S(1)} %pad_maximum_fusion.2), channel_id=1, source_target_pairs={{1,0},{2,1},{3,2},{0,3},{5,4},{6,5},{7,6},{4,7},{9,8},{10,9},{11,1... | collective-permute-start | bytes 2654216 | tf_op jit(solution)/shard_map/ppermute | solution.py:20
  289.0 22.5 %collective-permute-start.17 = (f32[3,3,1,4,48,128]{5,4,3,2,1,0:T(8,128)S(1)}, f32[3,3,1,4,48,128]{5,4,3,2,1,0:T(8,128)S(1)}, u32[]{:S(2)}, u32[]{:S(2)}) collective-permute-start(f32[3,3,1,4,48,128]{5,4,3,2,1,0:T(8,128)S(1)} %pad_maximum_fusion.2), channel_id=1, source_target_pairs={{0,1},{1,2},{2,3},{3,0},{4,5},{5,6},{6,7},{7,4},{8,9},{9,10},{10,1... | collective-permute-start | bytes 2654216 | tf_op jit(solution)/shard_map/ppermute | solution.py:19
  314.9 41.2 %collective-permute-start.19 = (f32[1,1,1,4,48,128]{5,4,3,2,1,0:T(8,128)S(1)}, f32[1,1,1,4,48,128]{5,4,3,2,1,0:T(8,128)S(1)}, u32[]{:S(2)}, u32[]{:S(2)}) collective-permute-start(f32[1,1,1,4,48,128]{5,4,3,2,1,0:T(8,128)S(1)} %get-tuple-element.30), channel_id=1, source_target_pairs={{0,8},{8,16},{16,24},{24,0},{1,9},{9,17},{17,25},{25,1},{2,10},{10... | collective-permute-start | bytes 294920 | tf_op jit(solution)/shard_map/ppermute | solution.py:19
  316.2 39.9 %collective-permute-start.18 = (f32[1,1,1,4,48,128]{5,4,3,2,1,0:T(8,128)S(1)}, f32[1,1,1,4,48,128]{5,4,3,2,1,0:T(8,128)S(1)}, u32[]{:S(2)}, u32[]{:S(2)}) collective-permute-start(f32[1,1,1,4,48,128]{5,4,3,2,1,0:T(8,128)S(1)} %get-tuple-element.30), channel_id=1, source_target_pairs={{8,0},{16,8},{24,16},{0,24},{9,1},{17,9},{25,17},{1,25},{10,2},{18... | collective-permute-start | bytes 294920 | tf_op jit(solution)/shard_map/ppermute | solution.py:20
  356.2 10.2 %collective-permute-start.21 = (f32[3,1,1,4,48,128]{5,4,3,2,1,0:T(8,128)S(1)}, f32[3,1,1,4,48,128]{5,4,3,2,1,0:T(8,128)S(1)}, u32[]{:S(2)}, u32[]{:S(2)}) collective-permute-start(f32[3,1,1,4,48,128]{5,4,3,2,1,0:T(8,128)S(1)} %pad_maximum_fusion.8), channel_id=1, source_target_pairs={{0,4},{4,0},{1,5},{5,1},{2,6},{6,2},{3,7},{7,3},{8,12},{12,8},{9,1... | collective-permute-start | bytes 884744 | tf_op jit(solution)/shard_map/ppermute | solution.py:19
  358.5 12.0 %collective-permute-start.20 = (f32[3,1,1,4,48,128]{5,4,3,2,1,0:T(8,128)S(1)}, f32[3,1,1,4,48,128]{5,4,3,2,1,0:T(8,128)S(1)}, u32[]{:S(2)}, u32[]{:S(2)}) collective-permute-start(f32[3,1,1,4,48,128]{5,4,3,2,1,0:T(8,128)S(1)} %pad_maximum_fusion.8), channel_id=1, source_target_pairs={{4,0},{0,4},{5,1},{1,5},{6,2},{2,6},{7,3},{3,7},{12,8},{8,12},{13,... | collective-permute-start | bytes 884744 | tf_op jit(solution)/shard_map/ppermute | solution.py:20
  370.6 19.5 %collective-permute-start.22 = (f32[3,3,1,4,48,128]{5,4,3,2,1,0:T(8,128)S(1)}, f32[3,3,1,4,48,128]{5,4,3,2,1,0:T(8,128)S(1)}, u32[]{:S(2)}, u32[]{:S(2)}) collective-permute-start(f32[3,3,1,4,48,128]{5,4,3,2,1,0:T(8,128)S(1)} %pad_maximum_fusion.3), channel_id=1, source_target_pairs={{1,0},{2,1},{3,2},{0,3},{5,4},{6,5},{7,6},{4,7},{9,8},{10,9},{11,1... | collective-permute-start | bytes 2654216 | tf_op jit(solution)/shard_map/ppermute | solution.py:20
  370.7 21.5 %collective-permute-start.23 = (f32[3,3,1,4,48,128]{5,4,3,2,1,0:T(8,128)S(1)}, f32[3,3,1,4,48,128]{5,4,3,2,1,0:T(8,128)S(1)}, u32[]{:S(2)}, u32[]{:S(2)}) collective-permute-start(f32[3,3,1,4,48,128]{5,4,3,2,1,0:T(8,128)S(1)} %pad_maximum_fusion.3), channel_id=1, source_target_pairs={{0,1},{1,2},{2,3},{3,0},{4,5},{5,6},{6,7},{7,4},{8,9},{9,10},{10,1... | collective-permute-start | bytes 2654216 | tf_op jit(solution)/shard_map/ppermute | solution.py:19
  395.6 7.3 %collective-permute-start.25 = (f32[1,1,1,4,48,128]{5,4,3,2,1,0:T(8,128)S(1)}, f32[1,1,1,4,48,128]{5,4,3,2,1,0:T(8,128)S(1)}, u32[]{:S(2)}, u32[]{:S(2)}) collective-permute-start(f32[1,1,1,4,48,128]{5,4,3,2,1,0:T(8,128)S(1)} %get-tuple-element.27), channel_id=1, source_target_pairs={{0,8},{8,16},{16,24},{24,0},{1,9},{9,17},{17,25},{25,1},{2,10},{10... | collective-permute-start | bytes 294920 | tf_op jit(solution)/shard_map/ppermute | solution.py:19
  398.3 5.8 %collective-permute-start.24 = (f32[1,1,1,4,48,128]{5,4,3,2,1,0:T(8,128)S(1)}, f32[1,1,1,4,48,128]{5,4,3,2,1,0:T(8,128)S(1)}, u32[]{:S(2)}, u32[]{:S(2)}) collective-permute-start(f32[1,1,1,4,48,128]{5,4,3,2,1,0:T(8,128)S(1)} %get-tuple-element.27), channel_id=1, source_target_pairs={{8,0},{16,8},{24,16},{0,24},{9,1},{17,9},{25,17},{1,25},{10,2},{18... | collective-permute-start | bytes 294920 | tf_op jit(solution)/shard_map/ppermute | solution.py:20
  404.0 48.7 %collective-permute-start.27 = (f32[3,1,1,4,48,128]{5,4,3,2,1,0:T(8,128)S(1)}, f32[3,1,1,4,48,128]{5,4,3,2,1,0:T(8,128)S(1)}, u32[]{:S(2)}, u32[]{:S(2)}) collective-permute-start(f32[3,1,1,4,48,128]{5,4,3,2,1,0:T(8,128)S(1)} %pad_maximum_fusion.9), channel_id=1, source_target_pairs={{0,4},{4,0},{1,5},{5,1},{2,6},{6,2},{3,7},{7,3},{8,12},{12,8},{9,1... | collective-permute-start | bytes 884744 | tf_op jit(solution)/shard_map/ppermute | solution.py:19
  406.1 46.6 %collective-permute-start.26 = (f32[3,1,1,4,48,128]{5,4,3,2,1,0:T(8,128)S(1)}, f32[3,1,1,4,48,128]{5,4,3,2,1,0:T(8,128)S(1)}, u32[]{:S(2)}, u32[]{:S(2)}) collective-permute-start(f32[3,1,1,4,48,128]{5,4,3,2,1,0:T(8,128)S(1)} %pad_maximum_fusion.9), channel_id=1, source_target_pairs={{4,0},{0,4},{5,1},{1,5},{6,2},{2,6},{7,3},{3,7},{12,8},{8,12},{13,... | collective-permute-start | bytes 884744 | tf_op jit(solution)/shard_map/ppermute | solution.py:20
  452.8 18.1 %collective-permute-start.28 = (f32[3,3,1,4,48,128]{5,4,3,2,1,0:T(8,128)S(1)}, f32[3,3,1,4,48,128]{5,4,3,2,1,0:T(8,128)S(1)}, u32[]{:S(2)}, u32[]{:S(2)}) collective-permute-start(f32[3,3,1,4,48,128]{5,4,3,2,1,0:T(8,128)S(1)} %pad_maximum_fusion.4), channel_id=1, source_target_pairs={{1,0},{2,1},{3,2},{0,3},{5,4},{6,5},{7,6},{4,7},{9,8},{10,9},{11,1... | collective-permute-start | bytes 2654216 | tf_op jit(solution)/shard_map/ppermute | solution.py:20
  452.9 22.7 %collective-permute-start.29 = (f32[3,3,1,4,48,128]{5,4,3,2,1,0:T(8,128)S(1)}, f32[3,3,1,4,48,128]{5,4,3,2,1,0:T(8,128)S(1)}, u32[]{:S(2)}, u32[]{:S(2)}) collective-permute-start(f32[3,3,1,4,48,128]{5,4,3,2,1,0:T(8,128)S(1)} %pad_maximum_fusion.4), channel_id=1, source_target_pairs={{0,1},{1,2},{2,3},{3,0},{4,5},{5,6},{6,7},{7,4},{8,9},{9,10},{10,1... | collective-permute-start | bytes 2654216 | tf_op jit(solution)/shard_map/ppermute | solution.py:19
  (2 other events, 1.8 us)
Sparse Core Ops, SparseCore 0:
  14.2 122.0 all-reduce.5
where the time goes:
time: 526 us
  waiting for transfers between devices  287 us (55%)
  blocking collectives  166 us (32%)
  starting transfers between devices  31.9 us (6%)
  matrix products  16.3 us (3%)
  between operations  14.7 us (3%)
  other arithmetic  7.22 us (1%)
    psum x4, blocking collectives, sweep_step(): lax.psum((first[:half] + first[half:], second[:half] - second[half:], pow...  166 us
    psum x1, waiting for transfers between devices, local(): cross = lax.psum(local_cross, ('ta', 'gz', 'xy'))  126 us
    ppermute x15, waiting for transfers between devices, with_halo(): after = lax.ppermute(initial, axis, down)  110 us
    ppermute x15, waiting for transfers between devices, with_halo(): before = lax.ppermute(last, axis, up)  51.3 us
    ppermute x15, starting transfers between devices, with_halo(): before = lax.ppermute(last, axis, up)  20.6 us
    ppermute x15, starting transfers between devices, with_halo(): after = lax.ppermute(initial, axis, down)  11.2 us
  transfers between devices with their start and end apart: 31, of which 25 were waited for; matrix products, arithmetic and copies ran while one was open for 1% of the time, Pallas kernels for 0%

commit v1 on v0

v1 whole, which is shorter than its diff:
```python
import math

import jax
import jax.numpy as jnp
from jax import lax
from jax.sharding import PartitionSpec as P

AXES = ("ta", "gz", "xy")
HIGH = lax.Precision.HIGHEST


def neighbours(x):
    forward, backward = [], []
    for dim, axis in enumerate(AXES):
        peers, length = lax.axis_size(axis), x.shape[dim]
        if peers == 1:
            forward.append(jnp.roll(x, -1, dim))
            backward.append(jnp.roll(x, 1, dim))
            continue
        up = [(i, (i + 1) % peers) for i in range(peers)]
        down = [(j, i) for i, j in up]
        first = lax.slice_in_dim(x, 0, 1, axis=dim)
        last = lax.slice_in_dim(x, length - 1, length, axis=dim)
        after = lax.ppermute(first, axis, down)
        before = after if peers == 2 and length == 1 else lax.ppermute(last, axis, up)
        if length > 1:
            after = jnp.concatenate([lax.slice_in_dim(x, 1, length, axis=dim), after], dim)
            before = jnp.concatenate([before, lax.slice_in_dim(x, 0, length - 1, axis=dim)], dim)
        forward.append(after)
        backward.append(before)
    forward.append(jnp.roll(x, -1, 3))
    backward.append(jnp.roll(x, 1, 3))
    return forward + backward


def fold(product, dof, half):
    top, low = product[..., :dof, :], product[..., dof:, :]
    parts = []
    for c in range(0, product.shape[-1], 2 * half):
        parts.append(top[..., c : c + half] - low[..., c + half : c + 2 * half])
        parts.append(top[..., c + half : c + 2 * half] + low[..., c : c + half])
    return jnp.concatenate(parts, -1)


def operate(matrix, field, half):
    dof = field.shape[4]
    stacked = jnp.concatenate([field] + neighbours(field), 4)
    product = jnp.einsum("tzxyok,tzxykc->tzxyoc", matrix, stacked, precision=HIGH)
    return fold(product, dof, half)


def reduce_doubling(x):
    for axis in reversed(AXES):
        peers = lax.axis_size(axis)
        if peers & (peers - 1):
            x = lax.psum(x, axis)
            continue
        bit = 1
        while bit < peers:
            x = x + lax.ppermute(x, axis, [(i, i ^ bit) for i in range(peers)])
            bit *= 2
    return x


def reduce_exchange(x):
    total = math.prod(lax.axis_size(a) for a in AXES)
    copies = jnp.broadcast_to(x[None], (total,) + x.shape)
    return jnp.sum(lax.all_to_all(copies, AXES, 0, 0, tiled=True), axis=0)


def swap(x, half):
    return jnp.concatenate([x[..., half:], x[..., :half]], -1)


def scale(alpha, x, half):
    re, im = alpha
    a = jnp.concatenate([re, re], -1)
    b = jnp.concatenate([-im, im], -1)
    return a * x + b * swap(x, half)


def products(k0, k1, k2, half):
    dims = tuple(range(k0.ndim - 1))
    s0, s1 = swap(k0, half), swap(k1, half)
    pairs = [(k1, k0), (k1, s0), (k2, k0), (k2, s0), (k2, k1), (k2, s1), (k1, k1), (k2, k2)]
    return jnp.stack([jnp.sum(a * b, axis=dims) for a, b in pairs])


def two_alphas(g, half):
    def inner(i):
        p, q = g[i], g[i + 1]
        return p[:half] + p[half:], q[:half] - q[half:]

    c10, c20, c21 = inner(0), inner(2), inner(4)
    n1, n2 = g[6][:half] + g[6][half:], g[7][:half] + g[7][half:]
    ar, ai = c10[0] / n1, c10[1] / n1
    a2 = ar * ar + ai * ai
    num_re = c10[0] - ar * n1 - (ar * c20[0] + ai * c20[1]) + a2 * c21[0]
    num_im = c10[1] - ai * n1 - (ar * c20[1] - ai * c20[0]) + a2 * c21[1]
    den = n1 - 2.0 * (ar * c21[0] + ai * c21[1]) + a2 * n2
    return (ar, ai), (num_re / den, num_im / den)


def local(links, eigvecs, eig_real, eig_imag, rhs):
    nev = eig_real.shape[0]
    half = rhs.shape[-1] // 2
    dof = rhs.shape[4]
    dirs = links.shape[4]
    lat = rhs.shape[:4]

    down = 2.0 ** -math.ceil(0.5 * math.log2(6 * dirs * dof))
    sign = jnp.where(jnp.arange(dirs) == 0, down, -down).astype(jnp.float32)
    matrix = links.reshape(lat + (dirs, dof, 2, dof)) * sign[:, None, None, None]
    matrix = matrix.transpose(0, 1, 2, 3, 6, 5, 4, 7).reshape(lat + (2 * dof, dirs * dof))

    rows = eigvecs.reshape(-1, 2 * nev)
    flat = rhs.reshape(-1, 2 * half)
    cross = jnp.dot(rows.T, flat, precision=HIGH, preferred_element_type=jnp.float32)
    proj = jnp.concatenate(
        [cross[:nev, :half] + cross[nev:, half:], cross[:nev, half:] - cross[nev:, :half]], 1
    )
    proj = reduce_doubling(proj)

    lifted = operate(matrix, eigvecs, nev)
    both = operate(matrix, jnp.concatenate([lifted, rhs], -1), half)

    proj_re, proj_im = proj[:, :half], proj[:, half:]
    denom = (eig_real * eig_real + eig_imag * eig_imag)[:, None]
    coef_re = (proj_re * eig_real[:, None] + proj_im * eig_imag[:, None]) / denom
    coef_im = (proj_im * eig_real[:, None] - proj_re * eig_imag[:, None]) / denom
    block = jnp.concatenate(
        [jnp.concatenate([coef_re, coef_im], 1), jnp.concatenate([-coef_im, coef_re], 1)], 0
    )
    up_block = block * (1.0 / down)

    def combine(field, weights):
        out = jnp.dot(
            field.reshape(-1, 2 * nev), weights, precision=HIGH, preferred_element_type=jnp.float32
        )
        return out.reshape(rhs.shape)

    start = combine(eigvecs, block)
    k0 = rhs - combine(lifted, up_block)
    k1 = both[..., 2 * nev :] - combine(both[..., : 2 * nev], up_block)
    k2 = operate(matrix, k1, half)
    gram = reduce_doubling(products(k0, k1, k2, half))
    k3 = operate(matrix, k2, half)
    k4 = operate(matrix, k3, half)
    a0, a1 = two_alphas(gram, half)

    def step(alpha, x, y):
        return x - scale(alpha, y, half)

    r1, s1, t1, u1 = (step(a0, x, y) for x, y in ((k0, k1), (k1, k2), (k2, k3), (k3, k4)))
    r2, s2, t2 = (step(a1, x, y) for x, y in ((r1, s1), (s1, t1), (t1, u1)))
    a2, a3 = two_alphas(reduce_exchange(products(r2, s2, t2, half)), half)
    r3, s3 = step(a2, r2, s2), step(a2, s2, t2)

    def grow(x, alpha, y):
        return x + down * scale(alpha, y, half)

    solution = grow(grow(grow(grow(start, a0, k0), a1, r1), a2, r2), a3, r3)
    return solution, step(a3, r3, s3)


def solution(mesh):
    field = P("ta", "gz", "xy", None, None, None)
    return jax.shard_map(
        local,
        mesh=mesh,
        in_specs=(field, field, P(), P(), field),
        out_specs=(field, field),
        check_vma=False,
    )
```

time: 526 us -> 123 us (0.23)
  waiting for transfers between devices: 287 us -> 43.5 us
  blocking collectives: 166 us -> 0 us
  local copies, waits for them, and re-layouts: 2.84 us -> 19.9 us
  between operations: 14.7 us -> 1.43 us
    psum x4 -> x0, blocking collectives: 166 us -> none  [sweep_step(): lax.psum((first[:half] + first[half:], second[:half] - second[half:], pow...]
    ppermute x30 -> x35, waiting for transfers between devices: 161 us -> 35.5 us  [the longest x10 16.1 us: reduce_doubling(): x = x + lax.ppermute(x, axis, [(i, i ^ bit) for i in range(peers)])]
    psum x1 -> x0, waiting for transfers between devices: 126 us -> none  [local(): cross = lax.psum(local_cross, ('ta', 'gz', 'xy'))]
    unnamed x7 -> x57, local copies, waits for them, and re-layouts: 1.62 us -> 9.9 us
    all_to_all x0 -> x1, waiting for transfers between devices: none -> 8.02 us  [reduce_exchange(): return jnp.sum(lax.all_to_all(copies, AXES, 0, 0, tiled=True), axis=0)]
    dot_general x12 -> x9, matrix products: 16.3 us -> 12.2 us  [the longest x5 9.88 us: operate(): jnp.einsum('tzxyok,tzxykc->tzxyoc', matrix, stacked, precision=HIGH)]
    ppermute x30 -> x35, starting transfers between devices: 31.8 us -> 32.7 us  [the longest x15 20.3 us: neighbours(): after = lax.ppermute(first, axis, down)]
  transfers between devices with their start and end apart: 31 -> 36, of which waited for: 25 -> 18; matrix products, arithmetic and copies ran while one was open for 1% -> 24% of each run, Pallas kernels for 0% -> 0%
where the time goes in v1:
time: 123 us; the launch traced here: 122 us
  waiting for transfers between devices  43.5 us (35%)
  starting transfers between devices  35.3 us (29%)
  local copies, waits for them, and re-layouts  19.9 us (16%)
  matrix products  12.2 us (10%)
  other arithmetic  9.7 us (8%)
  between operations  1.43 us (1%)
    ppermute x15, starting transfers between devices, neighbours(): after = lax.ppermute(first, axis, down)  20.3 us
    ppermute x10, waiting for transfers between devices, reduce_doubling(): x = x + lax.ppermute(x, axis, [(i, i ^ bit) for i in range(peers)])  16.1 us
    ppermute x10, waiting for transfers between devices, neighbours(): lax.ppermute(last, axis, up)  15 us
    unnamed x57, local copies, waits for them, and re-layouts  9.9 us
    dot_general x5, matrix products, operate(): jnp.einsum('tzxyok,tzxykc->tzxyoc', matrix, stacked, precision=HIGH)  9.88 us
    all_to_all x1, waiting for transfers between devices, reduce_exchange(): return jnp.sum(lax.all_to_all(copies, AXES, 0, 0, tiled=True), axis=0)  8.02 us
    ppermute x10, starting transfers between devices, reduce_doubling(): x = x + lax.ppermute(x, axis, [(i, i ^ bit) for i in range(peers)])  6.55 us
    ppermute x10, starting transfers between devices, neighbours(): lax.ppermute(last, axis, up)  5.82 us
  transfers between devices with their start and end apart: 36, of which 18 were waited for; matrix products, arithmetic and copies ran while one was open for 24% of the time, Pallas kernels for 0%

profile of v1, /device:TPU:0, one launch (start us, length us, event | category | flops | bytes accessed | tf_op | source)
XLA Modules:
  0.0 122.1 jit_solution(12265564505527320506)
XLA Ops:
  0.6 5.1 %collective-permute-start.5 = (f32[1,1,1,4,48,128]{5,4,3,2,1,0:T(8,128)}, f32[1,1,1,4,48,128]{5,4,3,2,1,0:T(8,128)}, u32[]{:S(2)}, u32[]{:S(2)}) collective-permute-start(f32[1,1,1,4,48,128]{5,4,3,2,1,0:T(8,128)} %param.6), channel_id=1, source_target_pairs={{8,0},{16,8},{24,16},{0,24},{9,1},{17,9},{25,17},{1,25},{10,2},{18... | collective-permute-start | bytes 294920 | tf_op jit(solution)/shard_map/ppermute | solution.py:24
  5.8 1.5 %collective-permute-start.6 = (f32[1,1,1,4,48,128]{5,4,3,2,1,0:T(8,128)}, f32[1,1,1,4,48,128]{5,4,3,2,1,0:T(8,128)}, u32[]{:S(2)}, u32[]{:S(2)}) collective-permute-start(f32[1,1,1,4,48,128]{5,4,3,2,1,0:T(8,128)} %param.6), channel_id=1, source_target_pairs={{4,0},{0,4},{5,1},{1,5},{6,2},{2,6},{7,3},{3,7},{12,8},{8,12},{13,... | collective-permute-start | bytes 294920 | tf_op jit(solution)/shard_map/ppermute | solution.py:24
  9.9 1.6 %fusion.127 = (f32[1,1,1,3,48,128]{5,4,3,2,1,0:T(8,128)}, f32[1,1,1,3,48,128]{5,4,3,2,1,0:T(8,128)}) fusion(f32[1,1,1,4,48,128]{5,4,3,2,1,0:T(8,128)} %param.6), kind=kLoop, calls=%fused_computation.317 | loop fusion | bytes 294912 | tf_op jit(solution)/shard_map/jit(_roll_static)/slice | solution.py:32
  11.6 4.1 %reshape.1283 = f32[1,1,1,4,9,48,2,48]{7,6,5,3,4,2,1,0:T(2,128)S(1)} reshape(f32[1,1,1,4,9,4608]{5,3,4,2,1,0:T(4,128)} %param.5) | data formatting | bytes 1327104 | tf_op jit(solution)/shard_map/reshape | solution.py:113
  18.1 1.5 %collective-permute-start.1 = (f32[64,128]{1,0:T(8,128)S(1)}, f32[64,128]{1,0:T(8,128)S(1)}, u32[]{:S(2)}, u32[]{:S(2)}) collective-permute-start(f32[64,128]{1,0:T(8,128)S(1)} %fusion.134), channel_id=1, source_target_pairs={{0,2},{1,3},{2,0},{3,1},{4,6},{5,7},{6,4},{7,5},{8,10},{9,11},{10,... | collective-permute-start | bytes 98312 | tf_op jit(solution)/shard_map/ppermute | solution.py:60
  19.6 2.4 %collective-permute-done.1 = f32[64,128]{1,0:T(8,128)S(1)} collective-permute-done((f32[64,128]{1,0:T(8,128)S(1)}, f32[64,128]{1,0:T(8,128)S(1)}, u32[]{:S(2)}, u32[]{:S(2)}) %collective-permute-start.1) | collective-permute-done | bytes 32800 | tf_op jit(solution)/shard_map/ppermute | solution.py:60
  27.7 1.5 %constant_dynamic-update-slice_fusion.5 = f32[1,1,1,4,432,128]{5,4,3,2,1,0:T(8,128)} fusion(f32[1,1,1,4,432,128]{5,4,3,2,1,0:T(8,128)} %constant_dynamic-update-slice_fusion.6, f32[1,1,1,4,48,128]{5,4,3,2,1,0:T(8,128)} %collective-permute-done.5), kind=kLoop, calls=%fused_computation.142 | loop fusion | bytes 196608
  29.2 1.5 %constant_dynamic-update-slice_fusion.4 = f32[1,1,1,4,432,128]{5,4,3,2,1,0:T(8,128)} fusion(f32[1,1,1,4,432,128]{5,4,3,2,1,0:T(8,128)} %constant_dynamic-update-slice_fusion.5, f32[1,1,1,4,48,128]{5,4,3,2,1,0:T(8,128)} %collective-permute-done.6), kind=kLoop, calls=%fused_computation.141 | loop fusion | bytes 196608
  30.8 1.5 %constant_dynamic-update-slice_fusion.3 = f32[1,1,1,4,432,128]{5,4,3,2,1,0:T(8,128)} fusion(f32[1,1,1,4,432,128]{5,4,3,2,1,0:T(8,128)} %constant_dynamic-update-slice_fusion.4, f32[1,1,1,4,48,128]{5,4,3,2,1,0:T(8,128)} %collective-permute-done.7), kind=kLoop, calls=%fused_computation.140 | loop fusion | bytes 196608
  33.0 1.5 %constant_dynamic-update-slice_fusion.2 = f32[1,1,1,4,432,128]{5,4,3,2,1,0:T(8,128)} fusion(f32[1,1,1,4,432,128]{5,4,3,2,1,0:T(8,128)} %maximum_dynamic-update-slice_fusion.3, f32[1,1,1,4,48,128]{5,4,3,2,1,0:T(8,128)} %collective-permute-done.8), kind=kLoop, calls=%fused_computation.139 | loop fusion | bytes 196608
  34.5 1.6 %constant_dynamic-update-slice_fusion.1 = f32[1,1,1,4,432,128]{5,4,3,2,1,0:T(8,128)} fusion(f32[1,1,1,4,432,128]{5,4,3,2,1,0:T(8,128)} %constant_dynamic-update-slice_fusion.2, f32[1,1,1,4,48,128]{5,4,3,2,1,0:T(8,128)} %collective-permute-done.6), kind=kLoop, calls=%fused_computation.138 | loop fusion | bytes 196608
  37.4 2.9 %convolution_bitcast_fusion.3 = f32[1,1,1,4,96,128]{5,4,3,2,1,0:T(8,128)S(1)} fusion(f32[4,96,432]{1,2,0:T(8,128)S(1)} %reshape.1284, f32[1,1,1,4,432,128]{5,4,3,2,1,0:T(8,128)} %maximum_dynamic-update-slice_fusion.2), kind=kOutput, calls=%fused_computation.8 | convolution fusion | flops 254803968 | bytes 1744896 | tf_op jit(solution)/shard_map/tzxyok,tzxykc->tzxyoc/dot_general | solution.py:48
  40.6 3.8 %collective-permute-start.10 = (f32[1,1,1,4,48,256]{5,4,3,2,1,0:T(8,128)S(1)}, f32[1,1,1,4,48,256]{5,4,3,2,1,0:T(8,128)S(1)}, u32[]{:S(2)}, u32[]{:S(2)}) collective-permute-start(f32[1,1,1,4,48,256]{5,4,3,2,1,0:T(8,128)S(1)} %get-tuple-element.44), channel_id=1, source_target_pairs={{8,0},{16,8},{24,16},{0,24},{9,1},{17,9},{25,17},{1,25},{10,2},{18... | collective-permute-start | bytes 589832 | tf_op jit(solution)/shard_map/ppermute | solution.py:24
  46.8 1.7 %collective-permute-start.13 = (f32[1,1,1,4,48,256]{5,4,3,2,1,0:T(8,128)S(1)}, f32[1,1,1,4,48,256]{5,4,3,2,1,0:T(8,128)S(1)}, u32[]{:S(2)}, u32[]{:S(2)}) collective-permute-start(f32[1,1,1,4,48,256]{5,4,3,2,1,0:T(8,128)S(1)} %get-tuple-element.44), channel_id=1, source_target_pairs={{0,8},{8,16},{16,24},{24,0},{1,9},{9,17},{17,25},{25,1},{2,10},{10... | collective-permute-start | bytes 589832 | tf_op jit(solution)/shard_map/ppermute | solution.py:25
  48.6 2.8 %collective-permute-done.4 = f32[64,128]{1,0:T(8,128)S(1)} collective-permute-done((f32[64,128]{1,0:T(8,128)S(1)}, f32[64,128]{1,0:T(8,128)S(1)}, u32[]{:S(2)}, u32[]{:S(2)}) %collective-permute-start.4) | collective-permute-done | bytes 32800 | tf_op jit(solution)/shard_map/ppermute | solution.py:60
  52.1 4.7 %collective-permute-done.13 = f32[1,1,1,4,48,256]{5,4,3,2,1,0:T(8,128)S(1)} collective-permute-done((f32[1,1,1,4,48,256]{5,4,3,2,1,0:T(8,128)S(1)}, f32[1,1,1,4,48,256]{5,4,3,2,1,0:T(8,128)S(1)}, u32[]{:S(2)}, u32[]{:S(2)}) %collective-permute-start.13) | collective-permute-done | bytes 196640 | tf_op jit(solution)/shard_map/ppermute | solution.py:25
  56.9 1.8 %fusion.3 = f32[1,1,1,4,96,256]{5,4,3,2,1,0:T(8,128)S(1)} fusion(f32[4,96,432]{1,2,0:T(8,128)S(1)} %reshape.1284, f32[1,1,1,4,432,256]{5,4,3,2,1,0:T(8,128)S(1)} %maximum_dynamic-update-slice_fusion), kind=kOutput, calls=%fused_computation.4 | convolution fusion | flops 509607936 | bytes 2826240 | tf_op jit(solution)/shard_map/tzxyok,tzxykc->tzxyoc/dot_general | solution.py:48
  59.2 3.7 %collective-permute-start.15 = (f32[1,1,1,4,48,128]{5,4,3,2,1,0:T(8,128)S(1)}, f32[1,1,1,4,48,128]{5,4,3,2,1,0:T(8,128)S(1)}, u32[]{:S(2)}, u32[]{:S(2)}) collective-permute-start(f32[1,1,1,4,48,128]{5,4,3,2,1,0:T(8,128)S(1)} %bitcast.323), channel_id=1, source_target_pairs={{8,0},{16,8},{24,16},{0,24},{9,1},{17,9},{25,17},{1,25},{10,2},{18... | collective-permute-start | bytes 294920 | tf_op jit(solution)/shard_map/ppermute | solution.py:24
  65.7 1.9 %collective-permute-done.16 = f32[1,1,1,4,48,128]{5,4,3,2,1,0:T(8,128)S(1)} collective-permute-done((f32[1,1,1,4,48,128]{5,4,3,2,1,0:T(8,128)S(1)}, f32[1,1,1,4,48,128]{5,4,3,2,1,0:T(8,128)S(1)}, u32[]{:S(2)}, u32[]{:S(2)}) %collective-permute-start.16) | collective-permute-done | bytes 98336 | tf_op jit(solution)/shard_map/ppermute | solution.py:24
  67.6 2.9 %collective-permute-done.18 = f32[1,1,1,4,48,128]{5,4,3,2,1,0:T(8,128)S(1)} collective-permute-done((f32[1,1,1,4,48,128]{5,4,3,2,1,0:T(8,128)S(1)}, f32[1,1,1,4,48,128]{5,4,3,2,1,0:T(8,128)S(1)}, u32[]{:S(2)}, u32[]{:S(2)}) %collective-permute-start.18) | collective-permute-done | bytes 98336 | tf_op jit(solution)/shard_map/ppermute | solution.py:25
  70.6 1.7 %convolution_bitcast_fusion.2 = f32[1,1,1,4,96,128]{5,4,3,2,1,0:T(8,128)S(1)} fusion(f32[4,96,432]{1,2,0:T(8,128)S(1)} %reshape.1284, f32[1,1,1,4,432,128]{5,4,3,2,1,0:T(8,128)S(1)} %maximum_dynamic-update-slice_fusion.4), kind=kOutput, calls=%fused_computation.7 | convolution fusion | flops 254803968 | bytes 1744896 | tf_op jit(solution)/shard_map/tzxyok,tzxykc->tzxyoc/dot_general | solution.py:48
  75.3 2.4 %collective-permute-done.21 = f32[8,128]{1,0:T(8,128)S(1)} collective-permute-done((f32[8,128]{1,0:T(8,128)S(1)}, f32[8,128]{1,0:T(8,128)S(1)}, u32[]{:S(2)}, u32[]{:S(2)}) %collective-permute-start.21) | collective-permute-done | bytes 4128 | tf_op jit(solution)/shard_map/ppermute | solution.py:60
  77.7 1.5 %collective-permute-start.22 = (f32[8,128]{1,0:T(8,128)S(1)}, f32[8,128]{1,0:T(8,128)S(1)}, u32[]{:S(2)}, u32[]{:S(2)}) collective-permute-start(f32[8,128]{1,0:T(8,128)S(1)} %add.319), channel_id=1, source_target_pairs={{0,4},{4,0},{1,5},{5,1},{2,6},{6,2},{3,7},{7,3},{8,12},{12,8},{9,1... | collective-permute-start | bytes 12296 | tf_op jit(solution)/shard_map/ppermute | solution.py:60
  82.3 2.6 %collective-permute-done.23 = f32[8,128]{1,0:T(8,128)S(1)} collective-permute-done((f32[8,128]{1,0:T(8,128)S(1)}, f32[8,128]{1,0:T(8,128)S(1)}, u32[]{:S(2)}, u32[]{:S(2)}) %collective-permute-start.23) | collective-permute-done | bytes 4128 | tf_op jit(solution)/shard_map/ppermute | solution.py:60
  86.5 3.3 %collective-permute-done.24 = f32[8,128]{1,0:T(8,128)S(1)} collective-permute-done((f32[8,128]{1,0:T(8,128)S(1)}, f32[8,128]{1,0:T(8,128)S(1)}, u32[]{:S(2)}, u32[]{:S(2)}) %collective-permute-start.24) | collective-permute-done | bytes 4128 | tf_op jit(solution)/shard_map/ppermute | solution.py:60
  91.5 2.4 %collective-permute-done.29 = f32[1,1,1,4,48,128]{5,4,3,2,1,0:T(8,128)S(1)} collective-permute-done((f32[1,1,1,4,48,128]{5,4,3,2,1,0:T(8,128)S(1)}, f32[1,1,1,4,48,128]{5,4,3,2,1,0:T(8,128)S(1)}, u32[]{:S(2)}, u32[]{:S(2)}) %collective-permute-start.29) | collective-permute-done | bytes 98336 | tf_op jit(solution)/shard_map/ppermute | solution.py:25
  93.9 1.7 %convolution_bitcast_fusion.1 = f32[1,1,1,4,96,128]{5,4,3,2,1,0:T(8,128)S(1)} fusion(f32[4,96,432]{1,2,0:T(8,128)S(1)} %reshape.1284, f32[1,1,1,4,432,128]{5,4,3,2,1,0:T(8,128)S(1)} %maximum_dynamic-update-slice_fusion.6), kind=kOutput, calls=%fused_computation.6 | convolution fusion | flops 254803968 | bytes 1744896 | tf_op jit(solution)/shard_map/tzxyok,tzxykc->tzxyoc/dot_general | solution.py:48
  96.5 1.5 %collective-permute-start.31 = (f32[1,1,1,4,48,128]{5,4,3,2,1,0:T(8,128)S(1)}, f32[1,1,1,4,48,128]{5,4,3,2,1,0:T(8,128)S(1)}, u32[]{:S(2)}, u32[]{:S(2)}) collective-permute-start(f32[1,1,1,4,48,128]{5,4,3,2,1,0:T(8,128)S(1)} %get-tuple-element.31), channel_id=1, source_target_pairs={{4,0},{0,4},{5,1},{1,5},{6,2},{2,6},{7,3},{3,7},{12,8},{8,12},{13,... | collective-permute-start | bytes 294920 | tf_op jit(solution)/shard_map/ppermute | solution.py:24
  101.2 4.0 %collective-permute-done.33 = f32[1,1,1,4,48,128]{5,4,3,2,1,0:T(8,128)S(1)} collective-permute-done((f32[1,1,1,4,48,128]{5,4,3,2,1,0:T(8,128)S(1)}, f32[1,1,1,4,48,128]{5,4,3,2,1,0:T(8,128)S(1)}, u32[]{:S(2)}, u32[]{:S(2)}) %collective-permute-start.33) | collective-permute-done | bytes 98336 | tf_op jit(solution)/shard_map/ppermute | solution.py:25
  105.3 1.7 %convolution_bitcast_fusion = f32[1,1,1,4,96,128]{5,4,3,2,1,0:T(8,128)S(1)} fusion(f32[4,96,432]{1,2,0:T(8,128)S(1)} %reshape.1284, f32[1,1,1,4,432,128]{5,4,3,2,1,0:T(8,128)S(1)} %maximum_dynamic-update-slice_fusion.8), kind=kOutput, calls=%fused_computation.5 | convolution fusion | flops 254803968 | bytes 1744896 | tf_op jit(solution)/shard_map/tzxyok,tzxykc->tzxyoc/dot_general | solution.py:48
  108.9 2.6 %all-to-all-start = ((f32[32,8,128]{2,1,0:T(8,128)}), f32[32,8,128]{2,1,0:T(8,128)S(1)}, u32[]{:S(2)}, u32[]{:S(2)}) async-start(f32[32,8,128]{2,1,0:T(8,128)} %broadcast_in_dim.12), calls=%async_computation | async-start | bytes 262144 | tf_op jit(solution)/shard_map/all_to_all | solution.py:68
  111.7 8.0 %all-to-all-done = f32[32,8,128]{2,1,0:T(8,128)S(1)} async-done(((f32[32,8,128]{2,1,0:T(8,128)}), f32[32,8,128]{2,1,0:T(8,128)S(1)}, u32[]{:S(2)}, u32[]{:S(2)}) %all-to-all-start) | async-done | bytes 131104 | tf_op jit(solution)/shard_map/all_to_all | solution.py:68
  (187 shorter events, 36.9 us)
Async XLA Ops:
  0.6 27.0 %collective-permute-start.5 = (f32[1,1,1,4,48,128]{5,4,3,2,1,0:T(8,128)}, f32[1,1,1,4,48,128]{5,4,3,2,1,0:T(8,128)}, u32[]{:S(2)}, u32[]{:S(2)}) collective-permute-start(f32[1,1,1,4,48,128]{5,4,3,2,1,0:T(8,128)} %param.6), channel_id=1, source_target_pairs={{8,0},{16,8},{24,16},{0,24},{9,1},{17,9},{25,17},{1,25},{10,2},{18... | collective-permute-start | bytes 294920 | tf_op jit(solution)/shard_map/ppermute | solution.py:24
  5.8 23.5 %collective-permute-start.6 = (f32[1,1,1,4,48,128]{5,4,3,2,1,0:T(8,128)}, f32[1,1,1,4,48,128]{5,4,3,2,1,0:T(8,128)}, u32[]{:S(2)}, u32[]{:S(2)}) collective-permute-start(f32[1,1,1,4,48,128]{5,4,3,2,1,0:T(8,128)} %param.6), channel_id=1, source_target_pairs={{4,0},{0,4},{5,1},{1,5},{6,2},{2,6},{7,3},{3,7},{12,8},{8,12},{13,... | collective-permute-start | bytes 294920 | tf_op jit(solution)/shard_map/ppermute | solution.py:24
  7.3 23.5 %collective-permute-start.7 = (f32[1,1,1,4,48,128]{5,4,3,2,1,0:T(8,128)}, f32[1,1,1,4,48,128]{5,4,3,2,1,0:T(8,128)}, u32[]{:S(2)}, u32[]{:S(2)}) collective-permute-start(f32[1,1,1,4,48,128]{5,4,3,2,1,0:T(8,128)} %param.6), channel_id=1, source_target_pairs={{1,0},{2,1},{3,2},{0,3},{5,4},{6,5},{7,6},{4,7},{9,8},{10,9},{11,1... | collective-permute-start | bytes 294920 | tf_op jit(solution)/shard_map/ppermute | solution.py:24
  7.7 25.3 %collective-permute-start.8 = (f32[1,1,1,4,48,128]{5,4,3,2,1,0:T(8,128)}, f32[1,1,1,4,48,128]{5,4,3,2,1,0:T(8,128)}, u32[]{:S(2)}, u32[]{:S(2)}) collective-permute-start(f32[1,1,1,4,48,128]{5,4,3,2,1,0:T(8,128)} %param.6), channel_id=1, source_target_pairs={{0,8},{8,16},{16,24},{24,0},{1,9},{9,17},{17,25},{25,1},{2,10},{10... | collective-permute-start | bytes 294920 | tf_op jit(solution)/shard_map/ppermute | solution.py:25
  9.8 7.4 %collective-permute-start = (f32[64,128]{1,0:T(8,128)}, f32[64,128]{1,0:T(8,128)}, u32[]{:S(2)}, u32[]{:S(2)}) collective-permute-start(f32[64,128]{1,0:T(8,128)} %pad_maximum_fusion.7), channel_id=1, source_target_pairs={{0,1},{1,0},{2,3},{3,2},{4,5},{5,4},{6,7},{7,6},{8,9},{9,8},{10,11... | collective-permute-start | bytes 98312 | tf_op jit(solution)/shard_map/ppermute | solution.py:60
  18.1 3.9 %collective-permute-start.1 = (f32[64,128]{1,0:T(8,128)S(1)}, f32[64,128]{1,0:T(8,128)S(1)}, u32[]{:S(2)}, u32[]{:S(2)}) collective-permute-start(f32[64,128]{1,0:T(8,128)S(1)} %fusion.134), channel_id=1, source_target_pairs={{0,2},{1,3},{2,0},{3,1},{4,6},{5,7},{6,4},{7,5},{8,10},{9,11},{10,... | collective-permute-start | bytes 98312 | tf_op jit(solution)/shard_map/ppermute | solution.py:60
  22.6 4.2 %collective-permute-start.2 = (f32[64,128]{1,0:T(8,128)}, f32[64,128]{1,0:T(8,128)}, u32[]{:S(2)}, u32[]{:S(2)}) collective-permute-start(f32[64,128]{1,0:T(8,128)} %add.308), channel_id=1, source_target_pairs={{0,4},{4,0},{1,5},{5,1},{2,6},{6,2},{3,7},{7,3},{8,12},{12,8},{9,1... | collective-permute-start | bytes 98312 | tf_op jit(solution)/shard_map/ppermute | solution.py:60
  26.8 9.3 %collective-permute-start.9 = (f32[1,1,1,4,48,128]{5,4,3,2,1,0:T(8,128)S(1)}, f32[1,1,1,4,48,128]{5,4,3,2,1,0:T(8,128)S(1)}, u32[]{:S(2)}, u32[]{:S(2)}) collective-permute-start(f32[1,1,1,4,48,128]{5,4,3,2,1,0:T(8,128)S(1)} %copy-done.1), channel_id=1, source_target_pairs={{0,1},{1,2},{2,3},{3,0},{4,5},{5,6},{6,7},{7,4},{8,9},{9,10},{10,1... | collective-permute-start | bytes 294920 | tf_op jit(solution)/shard_map/ppermute | solution.py:25
  27.6 18.5 %collective-permute-start.3 = (f32[64,128]{1,0:T(8,128)S(1)}, f32[64,128]{1,0:T(8,128)S(1)}, u32[]{:S(2)}, u32[]{:S(2)}) collective-permute-start(f32[64,128]{1,0:T(8,128)S(1)} %add.309), channel_id=1, source_target_pairs={{0,8},{8,0},{16,24},{24,16},{1,9},{9,1},{17,25},{25,17},{2,10},{10... | collective-permute-start | bytes 98312 | tf_op jit(solution)/shard_map/ppermute | solution.py:60
  40.6 11.4 %collective-permute-start.10 = (f32[1,1,1,4,48,256]{5,4,3,2,1,0:T(8,128)S(1)}, f32[1,1,1,4,48,256]{5,4,3,2,1,0:T(8,128)S(1)}, u32[]{:S(2)}, u32[]{:S(2)}) collective-permute-start(f32[1,1,1,4,48,256]{5,4,3,2,1,0:T(8,128)S(1)} %get-tuple-element.44), channel_id=1, source_target_pairs={{8,0},{16,8},{24,16},{0,24},{9,1},{17,9},{25,17},{1,25},{10,2},{18... | collective-permute-start | bytes 589832 | tf_op jit(solution)/shard_map/ppermute | solution.py:24
  44.4 7.7 %collective-permute-start.11 = (f32[1,1,1,4,48,256]{5,4,3,2,1,0:T(8,128)S(1)}, f32[1,1,1,4,48,256]{5,4,3,2,1,0:T(8,128)S(1)}, u32[]{:S(2)}, u32[]{:S(2)}) collective-permute-start(f32[1,1,1,4,48,256]{5,4,3,2,1,0:T(8,128)S(1)} %get-tuple-element.44), channel_id=1, source_target_pairs={{4,0},{0,4},{5,1},{1,5},{6,2},{2,6},{7,3},{3,7},{12,8},{8,12},{13,... | collective-permute-start | bytes 589832 | tf_op jit(solution)/shard_map/ppermute | solution.py:24
  44.9 7.2 %collective-permute-start.12 = (f32[1,1,1,4,48,256]{5,4,3,2,1,0:T(8,128)S(1)}, f32[1,1,1,4,48,256]{5,4,3,2,1,0:T(8,128)S(1)}, u32[]{:S(2)}, u32[]{:S(2)}) collective-permute-start(f32[1,1,1,4,48,256]{5,4,3,2,1,0:T(8,128)S(1)} %get-tuple-element.44), channel_id=1, source_target_pairs={{1,0},{2,1},{3,2},{0,3},{5,4},{6,5},{7,6},{4,7},{9,8},{10,9},{11,1... | collective-permute-start | bytes 589832 | tf_op jit(solution)/shard_map/ppermute | solution.py:24
  46.1 5.2 %collective-permute-start.4 = (f32[64,128]{1,0:T(8,128)S(1)}, f32[64,128]{1,0:T(8,128)S(1)}, u32[]{:S(2)}, u32[]{:S(2)}) collective-permute-start(f32[64,128]{1,0:T(8,128)S(1)} %add.310), channel_id=1, source_target_pairs={{0,16},{8,24},{16,0},{24,8},{1,17},{9,25},{17,1},{25,9},{2,18},{10... | collective-permute-start | bytes 98312 | tf_op jit(solution)/shard_map/ppermute | solution.py:60
  46.8 10.0 %collective-permute-start.13 = (f32[1,1,1,4,48,256]{5,4,3,2,1,0:T(8,128)S(1)}, f32[1,1,1,4,48,256]{5,4,3,2,1,0:T(8,128)S(1)}, u32[]{:S(2)}, u32[]{:S(2)}) collective-permute-start(f32[1,1,1,4,48,256]{5,4,3,2,1,0:T(8,128)S(1)} %get-tuple-element.44), channel_id=1, source_target_pairs={{0,8},{8,16},{16,24},{24,0},{1,9},{9,17},{17,25},{25,1},{2,10},{10... | collective-permute-start | bytes 589832 | tf_op jit(solution)/shard_map/ppermute | solution.py:25
  51.4 5.5 %collective-permute-start.14 = (f32[1,1,1,4,48,256]{5,4,3,2,1,0:T(8,128)S(1)}, f32[1,1,1,4,48,256]{5,4,3,2,1,0:T(8,128)S(1)}, u32[]{:S(2)}, u32[]{:S(2)}) collective-permute-start(f32[1,1,1,4,48,256]{5,4,3,2,1,0:T(8,128)S(1)} %get-tuple-element.44), channel_id=1, source_target_pairs={{0,1},{1,2},{2,3},{3,0},{4,5},{5,6},{6,7},{7,4},{8,9},{9,10},{10,1... | collective-permute-start | bytes 589832 | tf_op jit(solution)/shard_map/ppermute | solution.py:25
  59.2 6.5 %collective-permute-start.15 = (f32[1,1,1,4,48,128]{5,4,3,2,1,0:T(8,128)S(1)}, f32[1,1,1,4,48,128]{5,4,3,2,1,0:T(8,128)S(1)}, u32[]{:S(2)}, u32[]{:S(2)}) collective-permute-start(f32[1,1,1,4,48,128]{5,4,3,2,1,0:T(8,128)S(1)} %bitcast.323), channel_id=1, source_target_pairs={{8,0},{16,8},{24,16},{0,24},{9,1},{17,9},{25,17},{1,25},{10,2},{18... | collective-permute-start | bytes 294920 | tf_op jit(solution)/shard_map/ppermute | solution.py:24
  62.9 4.6 %collective-permute-start.16 = (f32[1,1,1,4,48,128]{5,4,3,2,1,0:T(8,128)S(1)}, f32[1,1,1,4,48,128]{5,4,3,2,1,0:T(8,128)S(1)}, u32[]{:S(2)}, u32[]{:S(2)}) collective-permute-start(f32[1,1,1,4,48,128]{5,4,3,2,1,0:T(8,128)S(1)} %bitcast.324), channel_id=1, source_target_pairs={{4,0},{0,4},{5,1},{1,5},{6,2},{2,6},{7,3},{3,7},{12,8},{8,12},{13,... | collective-permute-start | bytes 294920 | tf_op jit(solution)/shard_map/ppermute | solution.py:24
  63.5 4.1 %collective-permute-start.17 = (f32[1,1,1,4,48,128]{5,4,3,2,1,0:T(8,128)S(1)}, f32[1,1,1,4,48,128]{5,4,3,2,1,0:T(8,128)S(1)}, u32[]{:S(2)}, u32[]{:S(2)}) collective-permute-start(f32[1,1,1,4,48,128]{5,4,3,2,1,0:T(8,128)S(1)} %bitcast.325), channel_id=1, source_target_pairs={{1,0},{2,1},{3,2},{0,3},{5,4},{6,5},{7,6},{4,7},{9,8},{10,9},{11,1... | collective-permute-start | bytes 294920 | tf_op jit(solution)/shard_map/ppermute | solution.py:24
  63.5 7.1 %collective-permute-start.18 = (f32[1,1,1,4,48,128]{5,4,3,2,1,0:T(8,128)S(1)}, f32[1,1,1,4,48,128]{5,4,3,2,1,0:T(8,128)S(1)}, u32[]{:S(2)}, u32[]{:S(2)}) collective-permute-start(f32[1,1,1,4,48,128]{5,4,3,2,1,0:T(8,128)S(1)} %bitcast.327), channel_id=1, source_target_pairs={{0,8},{8,16},{16,24},{24,0},{1,9},{9,17},{17,25},{25,1},{2,10},{10... | collective-permute-start | bytes 294920 | tf_op jit(solution)/shard_map/ppermute | solution.py:25
  63.5 7.0 %collective-permute-start.19 = (f32[1,1,1,4,48,128]{5,4,3,2,1,0:T(8,128)S(1)}, f32[1,1,1,4,48,128]{5,4,3,2,1,0:T(8,128)S(1)}, u32[]{:S(2)}, u32[]{:S(2)}) collective-permute-start(f32[1,1,1,4,48,128]{5,4,3,2,1,0:T(8,128)S(1)} %bitcast.328), channel_id=1, source_target_pairs={{0,1},{1,2},{2,3},{3,0},{4,5},{5,6},{6,7},{7,4},{8,9},{9,10},{10,1... | collective-permute-start | bytes 294920 | tf_op jit(solution)/shard_map/ppermute | solution.py:25
  74.1 3.6 %collective-permute-start.21 = (f32[8,128]{1,0:T(8,128)S(1)}, f32[8,128]{1,0:T(8,128)S(1)}, u32[]{:S(2)}, u32[]{:S(2)}) collective-permute-start(f32[8,128]{1,0:T(8,128)S(1)} %add.318), channel_id=1, source_target_pairs={{0,2},{1,3},{2,0},{3,1},{4,6},{5,7},{6,4},{7,5},{8,10},{9,11},{10,... | collective-permute-start | bytes 12296 | tf_op jit(solution)/shard_map/ppermute | solution.py:60
  79.5 10.9 %collective-permute-start.25 = (f32[1,1,1,4,48,128]{5,4,3,2,1,0:T(8,128)S(1)}, f32[1,1,1,4,48,128]{5,4,3,2,1,0:T(8,128)S(1)}, u32[]{:S(2)}, u32[]{:S(2)}) collective-permute-start(f32[1,1,1,4,48,128]{5,4,3,2,1,0:T(8,128)S(1)} %get-tuple-element.33), channel_id=1, source_target_pairs={{8,0},{16,8},{24,16},{0,24},{9,1},{17,9},{25,17},{1,25},{10,2},{18... | collective-permute-start | bytes 294920 | tf_op jit(solution)/shard_map/ppermute | solution.py:24
  80.4 10.0 %collective-permute-start.26 = (f32[1,1,1,4,48,128]{5,4,3,2,1,0:T(8,128)S(1)}, f32[1,1,1,4,48,128]{5,4,3,2,1,0:T(8,128)S(1)}, u32[]{:S(2)}, u32[]{:S(2)}) collective-permute-start(f32[1,1,1,4,48,128]{5,4,3,2,1,0:T(8,128)S(1)} %get-tuple-element.33), channel_id=1, source_target_pairs={{4,0},{0,4},{5,1},{1,5},{6,2},{2,6},{7,3},{3,7},{12,8},{8,12},{13,... | collective-permute-start | bytes 294920 | tf_op jit(solution)/shard_map/ppermute | solution.py:24
  81.0 9.5 %collective-permute-start.27 = (f32[1,1,1,4,48,128]{5,4,3,2,1,0:T(8,128)S(1)}, f32[1,1,1,4,48,128]{5,4,3,2,1,0:T(8,128)S(1)}, u32[]{:S(2)}, u32[]{:S(2)}) collective-permute-start(f32[1,1,1,4,48,128]{5,4,3,2,1,0:T(8,128)S(1)} %get-tuple-element.33), channel_id=1, source_target_pairs={{1,0},{2,1},{3,2},{0,3},{5,4},{6,5},{7,6},{4,7},{9,8},{10,9},{11,1... | collective-permute-start | bytes 294920 | tf_op jit(solution)/shard_map/ppermute | solution.py:24
  85.0 4.9 %collective-permute-start.24 = (f32[8,128]{1,0:T(8,128)S(1)}, f32[8,128]{1,0:T(8,128)S(1)}, u32[]{:S(2)}, u32[]{:S(2)}) collective-permute-start(f32[8,128]{1,0:T(8,128)S(1)} %add.321), channel_id=1, source_target_pairs={{0,16},{8,24},{16,0},{24,8},{1,17},{9,25},{17,1},{25,9},{2,18},{10... | collective-permute-start | bytes 12296 | tf_op jit(solution)/shard_map/ppermute | solution.py:60
  85.0 6.5 %collective-permute-start.28 = (f32[1,1,1,4,48,128]{5,4,3,2,1,0:T(8,128)S(1)}, f32[1,1,1,4,48,128]{5,4,3,2,1,0:T(8,128)S(1)}, u32[]{:S(2)}, u32[]{:S(2)}) collective-permute-start(f32[1,1,1,4,48,128]{5,4,3,2,1,0:T(8,128)S(1)} %get-tuple-element.33), channel_id=1, source_target_pairs={{0,8},{8,16},{16,24},{24,0},{1,9},{9,17},{17,25},{25,1},{2,10},{10... | collective-permute-start | bytes 294920 | tf_op jit(solution)/shard_map/ppermute | solution.py:25
  89.9 4.0 %collective-permute-start.29 = (f32[1,1,1,4,48,128]{5,4,3,2,1,0:T(8,128)S(1)}, f32[1,1,1,4,48,128]{5,4,3,2,1,0:T(8,128)S(1)}, u32[]{:S(2)}, u32[]{:S(2)}) collective-permute-start(f32[1,1,1,4,48,128]{5,4,3,2,1,0:T(8,128)S(1)} %get-tuple-element.33), channel_id=1, source_target_pairs={{0,1},{1,2},{2,3},{3,0},{4,5},{5,6},{6,7},{7,4},{8,9},{9,10},{10,1... | collective-permute-start | bytes 294920 | tf_op jit(solution)/shard_map/ppermute | solution.py:25
  95.9 4.7 %collective-permute-start.30 = (f32[1,1,1,4,48,128]{5,4,3,2,1,0:T(8,128)S(1)}, f32[1,1,1,4,48,128]{5,4,3,2,1,0:T(8,128)S(1)}, u32[]{:S(2)}, u32[]{:S(2)}) collective-permute-start(f32[1,1,1,4,48,128]{5,4,3,2,1,0:T(8,128)S(1)} %get-tuple-element.31), channel_id=1, source_target_pairs={{8,0},{16,8},{24,16},{0,24},{9,1},{17,9},{25,17},{1,25},{10,2},{18... | collective-permute-start | bytes 294920 | tf_op jit(solution)/shard_map/ppermute | solution.py:24
  96.5 4.6 %collective-permute-start.31 = (f32[1,1,1,4,48,128]{5,4,3,2,1,0:T(8,128)S(1)}, f32[1,1,1,4,48,128]{5,4,3,2,1,0:T(8,128)S(1)}, u32[]{:S(2)}, u32[]{:S(2)}) collective-permute-start(f32[1,1,1,4,48,128]{5,4,3,2,1,0:T(8,128)S(1)} %get-tuple-element.31), channel_id=1, source_target_pairs={{4,0},{0,4},{5,1},{1,5},{6,2},{2,6},{7,3},{3,7},{12,8},{8,12},{13,... | collective-permute-start | bytes 294920 | tf_op jit(solution)/shard_map/ppermute | solution.py:24
  98.2 7.1 %collective-permute-start.33 = (f32[1,1,1,4,48,128]{5,4,3,2,1,0:T(8,128)S(1)}, f32[1,1,1,4,48,128]{5,4,3,2,1,0:T(8,128)S(1)}, u32[]{:S(2)}, u32[]{:S(2)}) collective-permute-start(f32[1,1,1,4,48,128]{5,4,3,2,1,0:T(8,128)S(1)} %get-tuple-element.31), channel_id=1, source_target_pairs={{0,8},{8,16},{16,24},{24,0},{1,9},{9,17},{17,25},{25,1},{2,10},{10... | collective-permute-start | bytes 294920 | tf_op jit(solution)/shard_map/ppermute | solution.py:25
  99.6 5.6 %collective-permute-start.34 = (f32[1,1,1,4,48,128]{5,4,3,2,1,0:T(8,128)S(1)}, f32[1,1,1,4,48,128]{5,4,3,2,1,0:T(8,128)S(1)}, u32[]{:S(2)}, u32[]{:S(2)}) collective-permute-start(f32[1,1,1,4,48,128]{5,4,3,2,1,0:T(8,128)S(1)} %get-tuple-element.31), channel_id=1, source_target_pairs={{0,1},{1,2},{2,3},{3,0},{4,5},{5,6},{6,7},{7,4},{8,9},{9,10},{10,1... | collective-permute-start | bytes 294920 | tf_op jit(solution)/shard_map/ppermute | solution.py:25
  108.9 10.8 %all-to-all-start = ((f32[32,8,128]{2,1,0:T(8,128)}), f32[32,8,128]{2,1,0:T(8,128)S(1)}, u32[]{:S(2)}, u32[]{:S(2)}) async-start(f32[32,8,128]{2,1,0:T(8,128)} %broadcast_in_dim.12), calls=%async_computation | async-start | bytes 262144 | tf_op jit(solution)/shard_map/all_to_all | solution.py:68
  (17 other events, 73.8 us)
